TPU v7x, 512 devices: a whole 4x8x8 slice. The times are simulated.
512 devices in a mesh: expert: 8 (over x, core), shard: 64 (over y, z).
Axes of the slice: x: 4, y: 8, z: 8, core: 2. Of those that a mesh axis runs over, the one named last changes fastest.
Arguments:
- tokens: bfloat16 [384, 4096], P('shard', 'expert'), may hold values from -6 to 6
- expert_ids: int32 [384, 2], P('shard'), may hold values from 0 to 7, all different within a row; in each aligned block of 6 rows (0 to 5, 6 to 11, ...) at most 3 rows name the same one
- gates: float32 [384, 2], P('shard'), may hold values from 0.1 to 1
- gate_proj: bfloat16 [8, 4096, 8192], P('expert', None, 'shard'), may hold values from -0.09375 to 0.09375
- up_proj: bfloat16 [8, 4096, 8192], P('expert', None, 'shard'), may hold values from -0.09375 to 0.09375
- down_proj_t: bfloat16 [8, 4096, 8192], P('expert', 'shard'), may hold values from -0.0625 to 0.0625
Outputs:
- mixed: bfloat16 [384, 4096], P('shard', 'expert')
Inputs may be any that keep to these rules, and one draw needn't show every extreme that they name: `expert_ids`: each token names two different experts; among the 6 tokens of one aligned block no expert is named more than 3 times, and in every draw some expert is named exactly 3 times in some block.
All inputs are finite; a program needn't handle non-finite values.
Results may differ from a plain program's by a relative error of at most 0.0085.
Values may be sent and summed in bfloat16 or wider, within the bound.
A program may use at most 64 MiB of HBM per device.

v0:
```python
import jax
import jax.numpy as jnp
from jax import lax
from jax.sharding import Mesh
from jax.sharding import PartitionSpec as P

SHARD = ("shard_0", "shard_1")


def in_order(parts, dim):
    parts = jnp.moveaxis(parts, 0, dim)
    lengths = parts.shape
    return parts.reshape(*lengths[:dim], lengths[dim] * lengths[dim + 1], *lengths[dim + 2 :])


def all_blocks(value, axes, turns):
    parts = value[None]
    for k in turns:
        parts = lax.all_gather(parts, axes[k], axis=0, tiled=True)
    held = [lax.axis_size(axes[k]) for k in reversed(turns)]
    parts = parts.reshape(*held, *value.shape)
    turned = sorted(range(len(turns)), key=lambda place: turns[len(turns) - 1 - place])
    return parts.transpose(*turned, *range(len(turns), parts.ndim)).reshape(-1, *value.shape)


def gathered_by_axis(value, axes, turns, dim):
    return in_order(all_blocks(value, axes, turns), dim)


def in_blocks(value, dim, length):
    before, after = (value.shape[:dim], value.shape[dim + 1 :])
    return jnp.moveaxis(value.reshape(*before, length, -1, *after), dim, 0)


def sum_at_owner(value, axis, dim):
    length = lax.axis_size(axis)
    parts = lax.all_to_all(in_blocks(value, dim, length), axis, 0, 0, tiled=True)
    return jnp.sum(parts.astype(jnp.float32), axis=0)


def shards(tokens, expert_ids, gates, gate_proj, up_proj, down_proj_t):
    experts = lax.axis_size("expert")
    tok_count = tokens.shape[0]
    capacity = min(tok_count, 4 * tok_count // experts)
    expert_range = jnp.arange(experts, dtype=jnp.int32)
    matches = expert_ids[:, :, None] == expert_range[None, None, :]
    routed = jnp.sum(matches.astype(jnp.int32), axis=1)
    weight = jnp.sum(gates[:, :, None] * matches.astype(jnp.float32), axis=1)
    slot_rank = jnp.cumsum(routed, axis=0) - routed
    slot_range = jnp.arange(capacity, dtype=jnp.int32)
    selector = (slot_rank.T[:, None, :] == slot_range[None, :, None]) & (routed.T[:, None, :] > 0)
    selector_bf = selector.astype(jnp.bfloat16)
    outgoing = jnp.einsum(
        "ect,td->ecd", selector_bf, tokens, preferred_element_type=jnp.float32
    ).astype(jnp.bfloat16)
    arrived = lax.all_to_all(outgoing, "expert", split_axis=0, concat_axis=2, tiled=True)
    own_rows = arrived[0]
    gate_local = gate_proj[0]
    up_local = up_proj[0]
    down_local = down_proj_t[0]
    piece = gathered_by_axis(own_rows, SHARD, (0, 1), 0)
    gate_out = jnp.dot(piece, gate_local, preferred_element_type=jnp.float32)
    up_out = jnp.dot(piece, up_local, preferred_element_type=jnp.float32)
    hidden = (jax.nn.silu(gate_out) * up_out).astype(jnp.bfloat16)
    down_rows = lax.all_to_all(down_local, SHARD, split_axis=1, concat_axis=0, tiled=True)
    expert_out = sum_at_owner(
        lax.dot_general(
            hidden, down_rows, (((1,), (1,)), ((), ())), preferred_element_type=jnp.float32
        ).astype(jnp.bfloat16),
        SHARD,
        0,
    ).astype(jnp.bfloat16)
    gathered_out = lax.all_to_all(expert_out, "expert", split_axis=1, concat_axis=0, tiled=True)
    combiner = (
        (selector.astype(jnp.float32) * weight.T[:, None, :])
        .reshape(experts * capacity, tok_count)
        .T
    )
    mixed_sum = jnp.dot(combiner, gathered_out.astype(jnp.float32), precision=lax.Precision.HIGHEST)
    return mixed_sum.astype(jnp.bfloat16)


def solution(mesh):
    split = Mesh(mesh.devices.reshape(mesh.shape["expert"], 8, 8), ("expert", "shard_0", "shard_1"))
    placed = (
        P(SHARD, "expert"),
        P(SHARD, None),
        P(SHARD, None),
        P("expert", None, SHARD),
        P("expert", None, SHARD),
        P("expert", SHARD, None),
    )
    return jax.shard_map(
        shards, mesh=split, in_specs=placed, out_specs=P(SHARD, "expert"), check_vma=False
    )
```

profile of v0, /device:TPU:24, one launch (start us, length us, event | category | flops | bytes accessed | tf_op | source)
XLA Modules:
  0.0 202.7 jit_solution(2765780398806376705)
XLA Ops:
  6.5 0.0 copy-start
  6.5 0.0 copy-start.1
  6.5 0.0 all-gather.2.cloned.1.call-start
  6.5 0.9 copy.27
  7.5 0.1 convert_reduce_fusion
  7.6 0.9 convolution_convert_fusion.1
  8.5 9.5 %all_to_all.58 = bf16[8,3,512]{2,1,0:T(4,128)(2,1)S(1)} all-to-all(bf16[8,3,512]{2,1,0:T(4,128)(2,1)S(1)} %copy.30), channel_id=1, replica_groups=mesh['expert'=8,'shard_0'=8,'shard_1'=8] {'expert'}, dimensions={0} | all-to-all | bytes 49152 | tf_op jit(solution)/shard_map/all_to_all | solution.py:56
  18.0 25.0 %all_gather.6 = bf16[8,3,4096]{2,1,0:T(4,128)(2,1)S(1)} all-gather(bf16[1,3,4096]{2,1,0:T(4,128)(2,1)S(1)} %bitcast.43), channel_id=1, replica_groups=mesh['expert'=8,'shard_0'=8,'shard_1'=8] {'shard_0'}, dimensions={0}, use_global_device_ids=true | all-gather | bytes 221184 | tf_op jit(solution)/shard_map/all_gather | solution.py:19
  43.1 0.8 copy.31
  43.9 0.0 all-gather.2.cloned.1.call-update
  43.9 0.0 copy-done.1
  43.9 0.3 copy.36
  44.2 1.7 copy.33
  45.9 16.5 %all-to-all-start.1 = ((bf16[64,64,128]{2,0,1:T(8,128)(2,1)}), bf16[64,64,128]{2,0,1:T(8,128)(2,1)}, u32[]{:S(2)}, u32[]{:S(2)}) async-start(bf16[64,64,128]{2,0,1:T(8,128)(2,1)} %copy.33), calls=%async_computation.1 | async-start | bytes 2097152 | tf_op jit(solution)/shard_map/all_to_all | solution.py:65
  62.4 44.6 %all-gather.2.cloned.1.call-done = bf16[64,3,4096]{2,0,1:T(8,128)(2,1)} async-done(((bf16[8,3,4096]{2,0,1:T(8,128)(2,1)}), bf16[64,3,4096]{2,0,1:T(8,128)(2,1)}) %all-gather.2.cloned.1.call-update) | async-done | bytes 1572880 | tf_op jit(solution)/shard_map/all_gather | solution.py:19
  107.0 4.1 %copy.32 = bf16[8,8,3,4096]{3,2,1,0:T(4,128)(2,1)} copy(bf16[8,8,3,4096]{3,0,1,2:T(8,128)(2,1)} %bitcast.41) | data formatting | bytes 3145728 | tf_op jit(solution)/shard_map/transpose | solution.py:23
  111.1 3.1 %reshape_reshape.3 = bf16[192,4096]{1,0:T(8,128)(2,1)S(1)} reshape(bf16[8,8,3,4096]{3,2,1,0:T(4,128)(2,1)} %copy.32) | data formatting | bytes 3145728 | tf_op jit(solution)/shard_map/reshape;reshape | solution.py:13
  114.2 1.8 fusion.4
  116.0 0.0 all-to-all-done.1
  116.0 0.0 copy-done
  116.1 3.4 %convolution_convert_fusion = bf16[192,4096]{1,0:T(8,128)(2,1)} fusion(bf16[4096,128]{1,0:T(8,128)(2,1)} %bitcast.12, bf16[192,4096]{1,0:T(8,128)(2,1)S(1)} %reshape_reshape.3, bf16[1,4096,128]{2,1,0:T(8,128)(2,1)S(1)} %copy-done, f32[192,128]{1,0:T(8,128)S(1)} %fusion.4), kind=kOutput, calls=%fused_computation | convolution fusion | flops 403587072 | bytes 5341184 | tf_op jit(solution)/shard_map/dot_general | solution.py:67
  119.5 4.1 %reshape.21 = bf16[64,3,4096]{2,1,0:T(4,128)(2,1)} reshape(bf16[192,4096]{1,0:T(8,128)(2,1)} %convolution_convert_fusion) | data formatting | bytes 3145728 | tf_op jit(solution)/shard_map/reshape | solution.py:32
  123.6 0.0 copy-start.2
  123.6 9.2 %all-to-all-start.2 = ((bf16[64,3,4096]{2,1,0:T(4,128)(2,1)}), bf16[64,3,4096]{2,1,0:T(4,128)(2,1)S(1)}, u32[]{:S(2)}, u32[]{:S(2)}) async-start(bf16[64,3,4096]{2,1,0:T(4,128)(2,1)} %reshape.21), calls=%async_computation.2 | async-start | bytes 4194304 | tf_op jit(solution)/shard_map/all_to_all | solution.py:37
  132.8 0.0 copy-done.2
  132.8 0.1 copy.28
  132.9 51.9 %all-to-all-done.2 = bf16[64,3,4096]{2,1,0:T(4,128)(2,1)S(1)} async-done(((bf16[64,3,4096]{2,1,0:T(4,128)(2,1)}), bf16[64,3,4096]{2,1,0:T(4,128)(2,1)S(1)}, u32[]{:S(2)}, u32[]{:S(2)}) %all-to-all-start.2) | async-done | bytes 1572896 | tf_op jit(solution)/shard_map/all_to_all | solution.py:37
  184.8 1.5 reduce_sum.32
  186.3 3.3 %all-to-all-start.3 = ((bf16[3,8,512]{2,0,1:T(4,128)(2,1)}), bf16[3,8,512]{2,0,1:T(4,128)(2,1)S(1)}, u32[]{:S(2)}, u32[]{:S(2)}) async-start(bf16[3,8,512]{2,0,1:T(4,128)(2,1)} %bitcast.13), calls=%async_computation.3 | async-start | bytes 65536 | tf_op jit(solution)/shard_map/all_to_all | solution.py:73
  189.7 0.1 select_reduce_fusion
  189.8 5.3 %all-to-all-done.3 = bf16[3,8,512]{2,0,1:T(4,128)(2,1)S(1)} async-done(((bf16[3,8,512]{2,0,1:T(4,128)(2,1)}), bf16[3,8,512]{2,0,1:T(4,128)(2,1)S(1)}, u32[]{:S(2)}, u32[]{:S(2)}) %all-to-all-start.3) | async-done | bytes 24608 | tf_op jit(solution)/shard_map/all_to_all | solution.py:73
  195.0 0.8 fusion.1
  (4 shorter events, 0.1 us)
Async XLA Ops:
  6.5 109.5 %copy-start = (bf16[1,4096,128]{2,1,0:T(8,128)(2,1)S(1)}, bf16[1,4096,128]{2,1,0:T(8,128)(2,1)}, u32[]{:S(2)}) copy-start(bf16[1,4096,128]{2,1,0:T(8,128)(2,1)} %param.10) | copy-start | bytes 3145732
  6.5 37.4 %copy-start.1 = (bf16[1,64,8192]{2,1,0:T(8,128)(2,1)S(1)}, bf16[1,64,8192]{2,1,0:T(8,128)(2,1)}, u32[]{:S(2)}) copy-start(bf16[1,64,8192]{2,1,0:T(8,128)(2,1)} %param.11) | copy-start | bytes 3145732
  6.5 100.4 %all-gather.2.cloned.1.call-start = ((), (), s32[]{:S(2)}) async-start(), calls=%async_computation.4 | async-start | bytes 1769472 | tf_op jit(solution)/shard_map/all_gather | solution.py:19
  45.9 70.1 %all-to-all-start.1 = ((bf16[64,64,128]{2,0,1:T(8,128)(2,1)}), bf16[64,64,128]{2,0,1:T(8,128)(2,1)}, u32[]{:S(2)}, u32[]{:S(2)}) async-start(bf16[64,64,128]{2,0,1:T(8,128)(2,1)} %copy.33), calls=%async_computation.1 | async-start | bytes 2097152 | tf_op jit(solution)/shard_map/all_to_all | solution.py:65
  123.6 9.2 %copy-start.2 = (f32[6,2]{0,1:T(2,128)S(1)}, f32[6,2]{0,1:T(2,128)}, u32[]{:S(2)}) copy-start(f32[6,2]{0,1:T(2,128)} %param.8) | copy-start | bytes 148
  123.6 61.3 %all-to-all-start.2 = ((bf16[64,3,4096]{2,1,0:T(4,128)(2,1)}), bf16[64,3,4096]{2,1,0:T(4,128)(2,1)S(1)}, u32[]{:S(2)}, u32[]{:S(2)}) async-start(bf16[64,3,4096]{2,1,0:T(4,128)(2,1)} %reshape.21), calls=%async_computation.2 | async-start | bytes 4194304 | tf_op jit(solution)/shard_map/all_to_all | solution.py:37
  186.3 8.7 %all-to-all-start.3 = ((bf16[3,8,512]{2,0,1:T(4,128)(2,1)}), bf16[3,8,512]{2,0,1:T(4,128)(2,1)S(1)}, u32[]{:S(2)}, u32[]{:S(2)}) async-start(bf16[3,8,512]{2,0,1:T(4,128)(2,1)} %bitcast.13), calls=%async_computation.3 | async-start | bytes 65536 | tf_op jit(solution)/shard_map/all_to_all | solution.py:73
Sparse Core Ops, SparseCore 0:
  44.0 62.9 all-gather.1
where the time goes:
time: 203 us
  waiting for transfers between devices  102 us (50%)
  blocking collectives  34.6 us (17%)
  starting transfers between devices  29 us (14%)
  local copies, waits for them, and re-layouts  15.1 us (7%)
  between operations  13.5 us (7%)
  matrix products  6.91 us (3%)
    all_to_all x1, waiting for transfers between devices, sum_at_owner(): lax.all_to_all(in_blocks(value, dim, length), axis, 0, 0, tiled=True)  51.9 us
    all_gather x1, waiting for transfers between devices, all_blocks(): parts = lax.all_gather(parts, axes[k], axis=0, tiled=True)  44.6 us
    all_gather x1, blocking collectives, all_blocks(): parts = lax.all_gather(parts, axes[k], axis=0, tiled=True)  25 us
    all_to_all x1, starting transfers between devices, shards(): lax.all_to_all(down_local, SHARD, split_axis=1, concat_axis=0, tiled=True)  16.5 us
    all_to_all x1, blocking collectives, shards(): lax.all_to_all(outgoing, 'expert', split_axis=0, concat_axis=2, tiled=True)  9.54 us
    all_to_all x1, starting transfers between devices, sum_at_owner(): lax.all_to_all(in_blocks(value, dim, length), axis, 0, 0, tiled=True)  9.21 us
    all_to_all x1, waiting for transfers between devices, shards(): lax.all_to_all(expert_out, 'expert', split_axis=1, concat_axis=0, tiled=T...  5.27 us
    transpose x1, local copies, waits for them, and re-layouts, all_blocks(): parts.transpose(*turned, *range(len(turns), parts.ndim))  4.11 us
  transfers between devices with their start and end apart: 4, of which 3 were waited for; matrix products, arithmetic and copies ran while one was open for 6% of the time, Pallas kernels for 0%

commit v1 on v0

--- a/solution.py
+++ b/solution.py
@@ -16,7 +16,8 @@
 def all_blocks(value, axes, turns):
     parts = value[None]
     for k in turns:
-        parts = lax.all_gather(parts, axes[k], axis=0, tiled=True)
+        outgoing_2 = jnp.stack([parts] * lax.axis_size(axes[k]))
+        parts = jnp.concatenate(lax.all_to_all(outgoing_2, axes[k], 0, 0), axis=0)
     held = [lax.axis_size(axes[k]) for k in reversed(turns)]
     parts = parts.reshape(*held, *value.shape)
     turned = sorted(range(len(turns)), key=lambda place: turns[len(turns) - 1 - place])

time: 203 us -> 196 us (0.966)
  waiting for transfers between devices: 102 us -> 118 us
  between operations: 13.5 us -> 0.09 us
  blocking collectives: 34.6 us -> 24.9 us
    all_gather x1 -> x0, waiting for transfers between devices: 44.6 us -> none  [all_blocks(): parts = lax.all_gather(parts, axes[k], axis=0, tiled=True)]
    all_to_all x0 -> x1, waiting for transfers between devices: none -> 35.7 us  [all_blocks(): parts = jnp.concatenate(lax.all_to_all(outgoing_2, axes[k], 0, 0), axis=0)]
    all_gather x1 -> x0, blocking collectives: 25 us -> none  [all_blocks(): parts = lax.all_gather(parts, axes[k], axis=0, tiled=True)]
    all_to_all x1, waiting for transfers between devices: 0.01 us -> 22.4 us  [shards(): lax.all_to_all(down_local, SHARD, split_axis=1, concat_axis=0, tiled=True)]
    all_to_all x0 -> x1, blocking collectives: none -> 15.4 us  [all_blocks(): parts = jnp.concatenate(lax.all_to_all(outgoing_2, axes[k], 0, 0), axis=0)]
    all_to_all x0 -> x1, starting transfers between devices: none -> 10.3 us  [all_blocks(): parts = jnp.concatenate(lax.all_to_all(outgoing_2, axes[k], 0, 0), axis=0)]
    all_to_all x1, starting transfers between devices: 16.5 us -> 7.84 us  [shards(): lax.all_to_all(down_local, SHARD, split_axis=1, concat_axis=0, tiled=True)]
    all_to_all x1, waiting for transfers between devices: 51.9 us -> 54.2 us  [sum_at_owner(): lax.all_to_all(in_blocks(value, dim, length), axis, 0, 0, tiled=True)]
  transfers between devices with their start and end apart: 4 -> 4, of which waited for: 3 -> 4; matrix products, arithmetic and copies ran while one was open for 6% -> 6% of each run, Pallas kernels for 0% -> 0%
where the time goes in v1:
time: 196 us
  waiting for transfers between devices  118 us (60%)
  starting transfers between devices  28.7 us (15%)
  blocking collectives  24.9 us (13%)
  local copies, waits for them, and re-layouts  15.6 us (8%)
  matrix products  6.92 us (4%)
    all_to_all x1, waiting for transfers between devices, sum_at_owner(): lax.all_to_all(in_blocks(value, dim, length), axis, 0, 0, tiled=True)  54.2 us
    all_to_all x1, waiting for transfers between devices, all_blocks(): parts = jnp.concatenate(lax.all_to_all(outgoing_2, axes[k], 0, 0), axis=0)  35.7 us
    all_to_all x1, waiting for transfers between devices, shards(): lax.all_to_all(down_local, SHARD, split_axis=1, concat_axis=0, tiled=True)  22.4 us
    all_to_all x1, blocking collectives, all_blocks(): parts = jnp.concatenate(lax.all_to_all(outgoing_2, axes[k], 0, 0), axis=0)  15.4 us
    all_to_all x1, starting transfers between devices, all_blocks(): parts = jnp.concatenate(lax.all_to_all(outgoing_2, axes[k], 0, 0), axis=0)  10.3 us
    all_to_all x1, blocking collectives, shards(): lax.all_to_all(outgoing, 'expert', split_axis=0, concat_axis=2, tiled=True)  9.54 us
    all_to_all x1, starting transfers between devices, shards(): lax.all_to_all(down_local, SHARD, split_axis=1, concat_axis=0, tiled=True)  7.84 us
    all_to_all x1, starting transfers between devices, sum_at_owner(): lax.all_to_all(in_blocks(value, dim, length), axis, 0, 0, tiled=True)  7.16 us
  transfers between devices with their start and end apart: 4, of which 4 were waited for; matrix products, arithmetic and copies ran while one was open for 6% of the time, Pallas kernels for 0%

profile of v1, /device:TPU:24, one launch (start us, length us, event | category | flops | bytes accessed | tf_op | source)
XLA Modules:
  0.0 195.5 jit_solution(15443216781769864980)
XLA Ops:
  0.0 0.0 copy-start
  0.0 0.9 copy.25
  0.9 0.1 convert_reduce_fusion
  1.0 0.9 convolution_convert_fusion.1
  1.9 9.5 %all_to_all.65 = bf16[8,3,512]{2,1,0:T(4,128)(2,1)S(1)} all-to-all(bf16[8,3,512]{2,1,0:T(4,128)(2,1)S(1)} %copy.28), channel_id=1, replica_groups=mesh['expert'=8,'shard_0'=8,'shard_1'=8] {'expert'}, dimensions={0} | all-to-all | bytes 49152 | tf_op jit(solution)/shard_map/all_to_all | solution.py:57
  11.5 0.1 stack.6
  11.5 15.4 %all_to_all.66 = bf16[8,1,3,4096]{3,2,1,0:T(4,128)(2,1)S(1)} all-to-all(bf16[8,1,3,4096]{3,2,1,0:T(4,128)(2,1)S(1)} %stack.6), channel_id=1, replica_groups=mesh['expert'=8,'shard_0'=8,'shard_1'=8] {'shard_0'}, dimensions={0} | all-to-all | bytes 393216 | tf_op jit(solution)/shard_map/all_to_all | solution.py:20
  26.9 0.1 copy.29
  27.1 1.3 stack.7
  28.4 10.3 %all-to-all-start.2 = ((bf16[8,8,3,4096]{3,1,2,0:T(8,128)(2,1)}), bf16[8,8,3,4096]{3,1,2,0:T(8,128)(2,1)S(1)}, u32[]{:S(2)}, u32[]{:S(2)}) async-start(bf16[8,8,3,4096]{3,1,2,0:T(8,128)(2,1)} %stack.7), calls=%async_computation.2 | async-start | bytes 3145728 | tf_op jit(solution)/shard_map/all_to_all | solution.py:20
  38.7 1.5 copy.34
  40.2 1.7 copy.31
  41.9 35.7 %all-to-all-done.2 = bf16[8,8,3,4096]{3,1,2,0:T(8,128)(2,1)S(1)} async-done(((bf16[8,8,3,4096]{3,1,2,0:T(8,128)(2,1)}), bf16[8,8,3,4096]{3,1,2,0:T(8,128)(2,1)S(1)}, u32[]{:S(2)}, u32[]{:S(2)}) %all-to-all-start.2) | async-done | bytes 1572896 | tf_op jit(solution)/shard_map/all_to_all | solution.py:20
  77.6 7.8 %all-to-all-start.3 = ((bf16[64,64,128]{2,0,1:T(8,128)(2,1)}), bf16[64,64,128]{2,0,1:T(8,128)(2,1)}, u32[]{:S(2)}, u32[]{:S(2)}) async-start(bf16[64,64,128]{2,0,1:T(8,128)(2,1)} %copy.31), calls=%async_computation.3 | async-start | bytes 2097152 | tf_op jit(solution)/shard_map/all_to_all | solution.py:66
  85.4 2.7 %copy.30 = bf16[8,8,3,4096]{3,2,1,0:T(4,128)(2,1)} copy(bf16[8,8,3,4096]{3,0,2,1:T(8,128)(2,1)S(1)} %bitcast.39) | data formatting | bytes 3145728 | tf_op jit(solution)/shard_map/transpose | solution.py:24
  88.1 3.1 %reshape_reshape.3 = bf16[192,4096]{1,0:T(8,128)(2,1)S(1)} reshape(bf16[8,8,3,4096]{3,2,1,0:T(4,128)(2,1)} %copy.30) | data formatting | bytes 3145728 | tf_op jit(solution)/shard_map/reshape;reshape | solution.py:13
  91.3 1.8 fusion.4
  93.1 22.4 %all-to-all-done.3 = bf16[64,64,128]{2,0,1:T(8,128)(2,1)} async-done(((bf16[64,64,128]{2,0,1:T(8,128)(2,1)}), bf16[64,64,128]{2,0,1:T(8,128)(2,1)}, u32[]{:S(2)}, u32[]{:S(2)}) %all-to-all-start.3) | async-done | bytes 1048608 | tf_op jit(solution)/shard_map/all_to_all | solution.py:66
  115.5 0.0 copy-done
  115.5 3.4 %convolution_convert_fusion = bf16[192,4096]{1,0:T(8,128)(2,1)} fusion(bf16[4096,128]{1,0:T(8,128)(2,1)} %bitcast.12, bf16[192,4096]{1,0:T(8,128)(2,1)S(1)} %reshape_reshape.3, bf16[1,4096,128]{2,1,0:T(8,128)(2,1)S(1)} %copy-done, f32[192,128]{1,0:T(8,128)S(1)} %fusion.4), kind=kOutput, calls=%fused_computation | convolution fusion | flops 403587072 | bytes 5341184 | tf_op jit(solution)/shard_map/dot_general | solution.py:68
  118.9 4.1 %reshape.24 = bf16[64,3,4096]{2,1,0:T(4,128)(2,1)} reshape(bf16[192,4096]{1,0:T(8,128)(2,1)} %convolution_convert_fusion) | data formatting | bytes 3145728 | tf_op jit(solution)/shard_map/reshape | solution.py:33
  123.0 0.0 copy-start.1
  123.0 7.2 %all-to-all-start.4 = ((bf16[64,3,4096]{2,1,0:T(4,128)(2,1)}), bf16[64,3,4096]{2,1,0:T(4,128)(2,1)S(1)}, u32[]{:S(2)}, u32[]{:S(2)}) async-start(bf16[64,3,4096]{2,1,0:T(4,128)(2,1)} %reshape.24), calls=%async_computation.4 | async-start | bytes 4194304 | tf_op jit(solution)/shard_map/all_to_all | solution.py:38
  130.2 0.0 copy-done.1
  130.2 0.1 copy.26
  130.3 54.2 %all-to-all-done.4 = bf16[64,3,4096]{2,1,0:T(4,128)(2,1)S(1)} async-done(((bf16[64,3,4096]{2,1,0:T(4,128)(2,1)}), bf16[64,3,4096]{2,1,0:T(4,128)(2,1)S(1)}, u32[]{:S(2)}, u32[]{:S(2)}) %all-to-all-start.4) | async-done | bytes 1572896 | tf_op jit(solution)/shard_map/all_to_all | solution.py:38
  184.5 1.5 reduce_sum.32
  186.0 3.3 %all-to-all-start.5 = ((bf16[3,8,512]{2,0,1:T(4,128)(2,1)}), bf16[3,8,512]{2,0,1:T(4,128)(2,1)S(1)}, u32[]{:S(2)}, u32[]{:S(2)}) async-start(bf16[3,8,512]{2,0,1:T(4,128)(2,1)} %bitcast.13), calls=%async_computation.5 | async-start | bytes 65536 | tf_op jit(solution)/shard_map/all_to_all | solution.py:74
  189.3 0.1 select_reduce_fusion
  189.4 5.3 %all-to-all-done.5 = bf16[3,8,512]{2,0,1:T(4,128)(2,1)S(1)} async-done(((bf16[3,8,512]{2,0,1:T(4,128)(2,1)}), bf16[3,8,512]{2,0,1:T(4,128)(2,1)S(1)}, u32[]{:S(2)}, u32[]{:S(2)}) %all-to-all-start.5) | async-done | bytes 24608 | tf_op jit(solution)/shard_map/all_to_all | solution.py:74
  194.7 0.8 fusion.1
  (4 shorter events, 0.1 us)
Async XLA Ops:
  0.0 115.5 %copy-start = (bf16[1,4096,128]{2,1,0:T(8,128)(2,1)S(1)}, bf16[1,4096,128]{2,1,0:T(8,128)(2,1)}, u32[]{:S(2)}) copy-start(bf16[1,4096,128]{2,1,0:T(8,128)(2,1)} %param.10) | copy-start | bytes 3145732
  28.4 49.2 %all-to-all-start.2 = ((bf16[8,8,3,4096]{3,1,2,0:T(8,128)(2,1)}), bf16[8,8,3,4096]{3,1,2,0:T(8,128)(2,1)S(1)}, u32[]{:S(2)}, u32[]{:S(2)}) async-start(bf16[8,8,3,4096]{3,1,2,0:T(8,128)(2,1)} %stack.7), calls=%async_computation.2 | async-start | bytes 3145728 | tf_op jit(solution)/shard_map/all_to_all | solution.py:20
  77.6 37.9 %all-to-all-start.3 = ((bf16[64,64,128]{2,0,1:T(8,128)(2,1)}), bf16[64,64,128]{2,0,1:T(8,128)(2,1)}, u32[]{:S(2)}, u32[]{:S(2)}) async-start(bf16[64,64,128]{2,0,1:T(8,128)(2,1)} %copy.31), calls=%async_computation.3 | async-start | bytes 2097152 | tf_op jit(solution)/shard_map/all_to_all | solution.py:66
  123.0 7.2 %copy-start.1 = (f32[6,2]{0,1:T(2,128)S(1)}, f32[6,2]{0,1:T(2,128)}, u32[]{:S(2)}) copy-start(f32[6,2]{0,1:T(2,128)} %param.8) | copy-start | bytes 148
  123.0 61.5 %all-to-all-start.4 = ((bf16[64,3,4096]{2,1,0:T(4,128)(2,1)}), bf16[64,3,4096]{2,1,0:T(4,128)(2,1)S(1)}, u32[]{:S(2)}, u32[]{:S(2)}) async-start(bf16[64,3,4096]{2,1,0:T(4,128)(2,1)} %reshape.24), calls=%async_computation.4 | async-start | bytes 4194304 | tf_op jit(solution)/shard_map/all_to_all | solution.py:38
  186.0 8.7 %all-to-all-start.5 = ((bf16[3,8,512]{2,0,1:T(4,128)(2,1)}), bf16[3,8,512]{2,0,1:T(4,128)(2,1)S(1)}, u32[]{:S(2)}, u32[]{:S(2)}) async-start(bf16[3,8,512]{2,0,1:T(4,128)(2,1)} %bitcast.13), calls=%async_computation.5 | async-start | bytes 65536 | tf_op jit(solution)/shard_map/all_to_all | solution.py:74
